TPU v7x, 32 devices: a whole 2x2x4 slice. The times are simulated.
32 devices in a mesh: ga: 8 (over y, x, core), ba: 4 (over z).
Axes of the slice: x: 2, y: 2, z: 4, core: 2. Of those that a mesh axis runs over, the one named last changes fastest.
Arguments:
- psi: float32 [2, 16384, 2048], P(None, 'ga', 'ba'), may hold values from -0.1875 to 0.1875
- dpsi: float32 [2, 16384, 512], P(None, 'ga', 'ba'), may hold values from -6 to 6
- band_weight: float32 [2048], replicated, may hold values from 0.25 to 1
- panel_band: int32 [16], P('ba'), may hold values from 0 to 15, each once
- slab_offset: int32 [8], replicated, may hold values from 0 to 2047
Outputs:
- projected: float32 [2, 16384, 512], P(None, 'ga', 'ba')
Inputs may be any that keep to these rules, and one draw needn't show every extreme that they name: panel_band is a permutation of the panel numbers.
All inputs are finite; a program needn't handle non-finite values.
Results may differ from a plain program's by a relative error of at most 0.00012.
Values sent between devices are 32-bit elements; how exact they have to be, the bound alone decides.
A program may use at most 128 MiB of HBM per device.

v0:
```python
import functools

import jax
import jax.numpy as jnp
from jax import lax
from jax.sharding import PartitionSpec as P

PANEL = 128


def tdot(left, right):
    return lax.dot_general(
        left,
        right,
        (((0,), (0,)), ((), ())),
        precision=lax.Precision.HIGH,
        preferred_element_type=jnp.float32,
    )


def mdot(left, right):
    return jnp.dot(left, right, precision=lax.Precision.HIGH, preferred_element_type=jnp.float32)


CHUNKS = 2


def turned(packed, width):
    column = lax.broadcasted_iota(jnp.int32, packed.shape, 1)
    first = (column // width) % 2 == 0
    return jnp.where(first, jnp.roll(packed, -width, axis=1), -jnp.roll(packed, width, axis=1))


def sum_over(block, axis, size):
    if size & (size - 1) or block.shape[0] % size:
        return lax.psum(block, axis)
    place = lax.axis_index(axis)
    bits = [1 << b for b in range(size.bit_length() - 1)]
    for bit in bits:
        upper = (place // bit) % 2
        half = block.shape[0] // 2
        kept = lax.dynamic_slice_in_dim(block, upper * half, half, 0)
        sent = lax.dynamic_slice_in_dim(block, (1 - upper) * half, half, 0)
        block = kept + lax.ppermute(sent, axis, [(i, i ^ bit) for i in range(size)])
    for bit in reversed(bits):
        upper = (place // bit) % 2 == 1
        other = lax.ppermute(block, axis, [(i, i ^ bit) for i in range(size)])
        block = jnp.concatenate([jnp.where(upper, other, block), jnp.where(upper, block, other)])
    return block


def weights_for(band_weight, panels):
    table = band_weight.reshape(-1, PANEL)
    onehot = (panels[:, None] == jnp.arange(table.shape[0], dtype=jnp.int32)[None, :]).astype(
        jnp.float32
    )
    return mdot(onehot, table).reshape(-1)


def per_device(size, psi, dpsi, band_weight, panel_band, slab_offset):
    offset = slab_offset[lax.axis_index("ga")]
    aligned = jnp.roll(dpsi, -offset, axis=1)
    local_weight = weights_for(band_weight, panel_band)
    width = aligned.shape[2] // CHUNKS
    owns, corrections = [], []
    for chunk in range(CHUNKS):
        columns = slice(chunk * width, (chunk + 1) * width)
        own = jnp.concatenate([aligned[0, :, columns], aligned[1, :, columns]], axis=1)
        every = lax.all_gather(own, "ba", axis=1, tiled=True)
        if corrections:
            every, corrections[-1] = lax.optimization_barrier((every, corrections[-1]))
        block = tdot(psi[0], every) + turned(tdot(psi[1], every), width)
        weighted = sum_over(block, "ga", size) * local_weight[:, None]
        owns.append(own)
        corrections.append(mdot(psi[0], weighted) - mdot(psi[1], turned(weighted, width)))
    pieces = [
        own - lax.psum_scatter(correction, "ba", scatter_dimension=1, tiled=True)
        for own, correction in zip(owns, corrections)
    ]
    result = jnp.stack(
        [
            jnp.concatenate([piece[:, part * width : (part + 1) * width] for piece in pieces], axis=1)
            for part in range(2)
        ]
    )
    return jnp.roll(result, offset, axis=1)


def solution(mesh):
    in_specs = (P(None, "ga", "ba"), P(None, "ga", "ba"), P(), P("ba"), P())
    out_specs = P(None, "ga", "ba")
    return jax.shard_map(
        functools.partial(per_device, mesh.shape["ga"]), mesh=mesh, in_specs=in_specs, out_specs=out_specs, check_vma=False
    )
```

profile of v0, /device:TPU:0, one launch (start us, length us, event | category | flops | bytes accessed | tf_op | source)
XLA Modules:
  0.0 346.7 jit_solution(5663664512739268655)
XLA Ops:
  6.5 1.2 dynamic_slice.42
  8.9 1.9 copy.6
  10.9 1.2 fusion.31
  12.2 1.0 pad_maximum_fusion
  13.4 1.0 pad_maximum_fusion.1
  14.5 82.4 %all-gather.5.cloned.1.call-done = f32[2048,512]{0,1:T(8,128)} async-done(((f32[2048,128]{0,1:T(8,128)}), f32[2048,512]{0,1:T(8,128)}) %all-gather.5.cloned.1.call-update) | async-done | bytes 4194320 | tf_op jit(solution)/shard_map/all_gather | solution.py:69
  96.9 6.5 %fusion.38 = f32[512,512]{1,0:T(8,128)S(1)} fusion(f32[2048,512]{0,1:T(8,128)} %all-gather.5.cloned.1.call-done, f32[2,2048,512]{2,1,0:T(8,128)} %param.7), kind=kOutput, calls=%fused_computation.43 | convolution fusion | flops 3221225472 | bytes 9437184 | tf_op jit(solution)/shard_map/dot_general | solution.py:12
  104.0 2.1 copy-done.3
  106.1 6.0 %fusion.47 = f32[512,512]{1,0:T(8,128)S(1)} fusion(f32[2048,512]{0,1:T(8,128)S(1)} %copy-done.3, f32[2,2048,512]{2,1,0:T(8,128)} %param.7, f32[512,64]{1,0:T(8,128)S(1)} %get-tuple-element.35, f32[512,448]{1,0:T(8,128)S(1)} %get-tuple-element.37, f32[512,448]{1,0:T(8,128)S(1)} %get-tuple-element.36, f32[512,64]{1,0:T(8,128)S(1)} %get-tuple-element.34, ...), kind=kOutput, calls=%fused_computation.46 | convolution fusion | flops 3225944064 | bytes 11538944 | tf_op jit(solution)/shard_map/dot_general | solution.py:12
  112.0 0.8 constant_dynamic-slice_fusion.5
  112.9 2.2 collective-permute-done
  115.2 1.2 dynamic-slice_add_fusion.1
  116.3 0.8 copy-done.4
  117.1 1.6 collective-permute-start.1
  118.7 6.9 %collective-permute-done.1 = f32[128,512]{1,0:T(8,128)S(1)} collective-permute-done((f32[128,512]{1,0:T(8,128)S(1)}, f32[128,512]{1,0:T(8,128)S(1)}, u32[]{:S(2)}, u32[]{:S(2)}) %collective-permute-start.1) | collective-permute-done | bytes 262176 | tf_op jit(solution)/shard_map/ppermute | solution.py:44
  125.5 1.0 dynamic-slice_add_fusion.3
  126.6 1.6 collective-permute-start.2
  128.1 3.5 %collective-permute-done.2 = f32[64,512]{1,0:T(8,128)S(1)} collective-permute-done((f32[64,512]{1,0:T(8,128)S(1)}, f32[64,512]{1,0:T(8,128)S(1)}, u32[]{:S(2)}, u32[]{:S(2)}) %collective-permute-start.2) | collective-permute-done | bytes 131104 | tf_op jit(solution)/shard_map/ppermute | solution.py:44
  131.6 1.6 collective-permute-start.3
  133.2 3.5 %collective-permute-done.3 = f32[64,512]{1,0:T(8,128)S(1)} collective-permute-done((f32[64,512]{1,0:T(8,128)S(1)}, f32[64,512]{1,0:T(8,128)S(1)}, u32[]{:S(2)}, u32[]{:S(2)}) %collective-permute-start.3) | collective-permute-done | bytes 131104 | tf_op jit(solution)/shard_map/ppermute | solution.py:47
  136.7 1.6 collective-permute-start.4
  138.3 4.9 %collective-permute-done.4 = f32[128,512]{1,0:T(8,128)S(1)} collective-permute-done((f32[128,512]{1,0:T(8,128)S(1)}, f32[128,512]{1,0:T(8,128)S(1)}, u32[]{:S(2)}, u32[]{:S(2)}) %collective-permute-start.4) | collective-permute-done | bytes 262176 | tf_op jit(solution)/shard_map/ppermute | solution.py:47
  143.2 0.8 pad_maximum_fusion.2
  144.2 1.9 collective-permute-done.5
  146.6 0.4 fusion.78
  147.0 9.8 %fusion.4 = f32[512,2048]{1,0:T(8,128)S(1)} fusion(f32[2,2048,512]{2,1,0:T(8,128)} %param.7, f32[512,64]{1,0:T(8,128)S(1)} %get-tuple-element.29, f32[512,448]{1,0:T(8,128)S(1)} %get-tuple-element.31, f32[512,448]{1,0:T(8,128)S(1)} %get-tuple-element.30, f32[512,64]{1,0:T(8,128)S(1)} %get-tuple-element.28, s32[512]{0:T(512)S(1)} %iota_shift-right-logical_fusion, ...), kind=kOutput, calls=%fused_computation.10 | convolution fusion | flops 3225681920 | bytes 10490368 | tf_op jit(solution)/shard_map/dot_general | solution.py:22
  156.8 8.9 %subtract_bitcast_fusion.1 = f32[2048,512]{0,1:T(8,128)} fusion(f32[512,2048]{1,0:T(8,128)S(1)} %fusion.4, f32[512,512]{1,0:T(8,128)S(1)} %maximum_multiply_fusion, f32[2,2048,512]{2,1,0:T(8,128)S(1)} %bitcast.75), kind=kOutput, calls=%fused_computation.23 | convolution fusion | flops 3222274048 | bytes 13631488 | tf_op jit(solution)/shard_map/dot_general | solution.py:22
  165.7 12.1 %all-gather.3.cloned.1.call-done = f32[2048,512]{0,1:T(8,128)} async-done(((f32[2048,128]{0,1:T(8,128)}), f32[2048,512]{0,1:T(8,128)}) %all-gather.3.cloned.1.call-update) | async-done | bytes 4194320 | tf_op jit(solution)/shard_map/all_gather | solution.py:69
  177.8 6.5 %fusion.41 = f32[512,512]{1,0:T(8,128)S(1)} fusion(f32[2048,512]{0,1:T(8,128)} %all-gather.3.cloned.1.call-done, f32[2,2048,512]{2,1,0:T(8,128)} %param.7), kind=kOutput, calls=%fused_computation.44 | convolution fusion | flops 3221225472 | bytes 9437184 | tf_op jit(solution)/shard_map/dot_general | solution.py:12
  184.9 2.0 copy-done.2
  186.9 6.0 %fusion.44 = f32[512,512]{1,0:T(8,128)S(1)} fusion(f32[2048,512]{0,1:T(8,128)S(1)} %copy-done.2, f32[2,2048,512]{2,1,0:T(8,128)} %param.7, f32[512,64]{1,0:T(8,128)S(1)} %get-tuple-element.25, f32[512,448]{1,0:T(8,128)S(1)} %get-tuple-element.27, f32[512,448]{1,0:T(8,128)S(1)} %get-tuple-element.26, f32[512,64]{1,0:T(8,128)S(1)} %get-tuple-element.24, ...), kind=kOutput, calls=%fused_computation.45 | convolution fusion | flops 3225944064 | bytes 11538944 | tf_op jit(solution)/shard_map/dot_general | solution.py:12
  193.1 1.9 collective-permute-done.6
  195.1 1.7 collective-permute-start.7
  196.8 6.7 %collective-permute-done.7 = f32[128,512]{1,0:T(8,128)S(1)} collective-permute-done((f32[128,512]{1,0:T(8,128)S(1)}, f32[128,512]{1,0:T(8,128)S(1)}, u32[]{:S(2)}, u32[]{:S(2)}) %collective-permute-start.7) | collective-permute-done | bytes 262176 | tf_op jit(solution)/shard_map/ppermute | solution.py:44
  203.6 1.7 collective-permute-start.8
  205.3 3.3 collective-permute-done.8
  208.6 1.7 collective-permute-start.9
  210.3 3.3 collective-permute-done.9
  213.7 1.7 collective-permute-start.10
  215.4 4.7 %collective-permute-done.10 = f32[128,512]{1,0:T(8,128)S(1)} collective-permute-done((f32[128,512]{1,0:T(8,128)S(1)}, f32[128,512]{1,0:T(8,128)S(1)}, u32[]{:S(2)}, u32[]{:S(2)}) %collective-permute-start.10) | collective-permute-done | bytes 262176 | tf_op jit(solution)/shard_map/ppermute | solution.py:47
  220.3 1.9 collective-permute-done.11
  223.0 7.5 %fusion = f32[512,2048]{1,0:T(8,128)S(1)} fusion(f32[2,2048,512]{2,1,0:T(8,128)S(1)} %bitcast.77, f32[512,64]{1,0:T(8,128)S(1)} %get-tuple-element.19, f32[512,448]{1,0:T(8,128)S(1)} %get-tuple-element.21, f32[512,448]{1,0:T(8,128)S(1)} %get-tuple-element.20, f32[512,64]{1,0:T(8,128)S(1)} %get-tuple-element.18, s32[512]{0:T(512)S(1)} %iota_shift-right-logical_fusion, ...), kind=kOutput, calls=%fused_computation.6 | convolution fusion | flops 3225681920 | bytes 11014656 | tf_op jit(solution)/shard_map/dot_general | solution.py:22
  230.5 8.6 %subtract_bitcast_fusion = f32[2048,512]{0,1:T(8,128)} fusion(f32[512,2048]{1,0:T(8,128)S(1)} %fusion, f32[512,512]{1,0:T(8,128)S(1)} %maximum_multiply_fusion.1, f32[2,2048,512]{2,1,0:T(8,128)S(1)} %bitcast.77), kind=kOutput, calls=%fused_computation.22 | convolution fusion | flops 3222274048 | bytes 13631488 | tf_op jit(solution)/shard_map/dot_general | solution.py:22
  240.3 15.1 %reduce-scatter.3.cloned.1.call-done = f32[2048,128]{0,1:T(8,128)} async-done(((f32[2048,512]{0,1:T(8,128)}), f32[2048,128]{0,1:T(8,128)}) %reduce-scatter.3.cloned.1.call-update) | async-done | bytes 1048592 | tf_op jit(solution)/shard_map/reduce_scatter | solution.py:77
  255.4 79.5 %reduce-scatter.5.cloned.1.call-done = f32[2048,128]{0,1:T(8,128)} async-done(((f32[2048,512]{0,1:T(8,128)}), f32[2048,128]{0,1:T(8,128)}) %reduce-scatter.5.cloned.1.call-update) | async-done | bytes 1048592 | tf_op jit(solution)/shard_map/reduce_scatter | solution.py:77
  334.9 2.0 fusion.67
  337.2 1.2 fusion.29
  338.3 1.8 copy.10
  (67 shorter events, 3.7 us)
Async XLA Ops:
  6.5 137.5 %copy-start = (f32[2048]{0:T(1024)S(1)}, f32[2048]{0:T(1024)}, u32[]{:S(2)}) copy-start(f32[2048]{0:T(1024)} %param.9) | copy-start | bytes 24580
  6.5 90.4 %all-gather.5.cloned.1.call-start = ((), (), s32[]{:S(2)}) async-start(), calls=%async_computation.3 | async-start | bytes 5242880 | tf_op jit(solution)/shard_map/all_gather | solution.py:69
  13.3 164.4 %all-gather.3.cloned.1.call-start = ((), (), s32[]{:S(2)}) async-start(), calls=%async_computation.2 | async-start | bytes 5242880 | tf_op jit(solution)/shard_map/all_gather | solution.py:69
  14.4 240.9 %reduce-scatter.3.cloned.1.call-start = ((), (), s32[]{:S(2)}) async-start(), calls=%async_computation.4 | async-start | bytes 5242880 | tf_op jit(solution)/shard_map/reduce_scatter | solution.py:77
  103.5 2.6 copy-start.3
  112.0 32.0 %copy-start.5 = (s32[4]{0:T(128)S(1)}, s32[4]{0:T(128)}, u32[]{:S(2)}) copy-start(s32[4]{0:T(128)} %param.10) | copy-start | bytes 52
  112.9 2.3 collective-permute-start
  116.3 0.8 copy-start.4
  117.1 8.4 %collective-permute-start.1 = (f32[128,512]{1,0:T(8,128)S(1)}, f32[128,512]{1,0:T(8,128)S(1)}, u32[]{:S(2)}, u32[]{:S(2)}) collective-permute-start(f32[128,512]{1,0:T(8,128)S(1)} %constant_dynamic-slice_fusion.4), channel_id=1, source_target_pairs={{0,8},{4,12},{8,0},{12,4},{16,24},{20,28},{24,16},{28,20},{1,9},{5... | collective-permute-start | bytes 786440 | tf_op jit(solution)/shard_map/ppermute | solution.py:44
  126.6 5.0 %collective-permute-start.2 = (f32[64,512]{1,0:T(8,128)S(1)}, f32[64,512]{1,0:T(8,128)S(1)}, u32[]{:S(2)}, u32[]{:S(2)}) collective-permute-start(f32[64,512]{1,0:T(8,128)S(1)} %constant_dynamic-slice_fusion.3), channel_id=1, source_target_pairs={{0,16},{4,20},{8,24},{12,28},{16,0},{20,4},{24,8},{28,12},{1,17},{... | collective-permute-start | bytes 393224 | tf_op jit(solution)/shard_map/ppermute | solution.py:44
  131.6 5.0 %collective-permute-start.3 = (f32[64,512]{1,0:T(8,128)S(1)}, f32[64,512]{1,0:T(8,128)S(1)}, u32[]{:S(2)}, u32[]{:S(2)}) collective-permute-start(f32[64,512]{1,0:T(8,128)S(1)} %dynamic-slice_add_fusion.5), channel_id=1, source_target_pairs={{0,16},{4,20},{8,24},{12,28},{16,0},{20,4},{24,8},{28,12},{1,17},{... | collective-permute-start | bytes 393224 | tf_op jit(solution)/shard_map/ppermute | solution.py:47
  136.7 6.4 %collective-permute-start.4 = (f32[128,512]{1,0:T(8,128)S(1)}, f32[128,512]{1,0:T(8,128)S(1)}, u32[]{:S(2)}, u32[]{:S(2)}) collective-permute-start(f32[128,512]{1,0:T(8,128)S(1)} %pad_maximum_fusion.4), channel_id=1, source_target_pairs={{0,8},{4,12},{8,0},{12,4},{16,24},{20,28},{24,16},{28,20},{1,9},{5... | collective-permute-start | bytes 786440 | tf_op jit(solution)/shard_map/ppermute | solution.py:47
  144.0 2.1 collective-permute-start.5
  146.6 10.2 %slice-start = ((s8[8388608]{0:T(1024)(128)(4,1)}), s8[4194304]{0:T(1024)(128)(4,1)S(1)}, s32[]{:S(2)}) async-start(s8[8388608]{0:T(1024)(128)(4,1)} %bitcast.74), calls=%async_computation.6 | async-start | bytes 8388608
  147.0 9.8 %slice-start.1 = ((s8[8388608]{0:T(1024)(128)(4,1)}), s8[4194304]{0:T(1024)(128)(4,1)S(1)}, s32[]{:S(2)}) async-start(s8[8388608]{0:T(1024)(128)(4,1)} %bitcast.74), calls=%async_computation.7 | async-start | bytes 8388608
  177.8 157.1 %reduce-scatter.5.cloned.1.call-start = ((), (), s32[]{:S(2)}) async-start(), calls=%async_computation.5 | async-start | bytes 5242880 | tf_op jit(solution)/shard_map/reduce_scatter | solution.py:77
  184.4 2.6 copy-start.2
  193.0 2.0 collective-permute-start.6
  194.9 28.0 %slice-start.2 = ((s8[8388608]{0:T(1024)(128)(4,1)}), s8[4194304]{0:T(1024)(128)(4,1)S(1)}, s32[]{:S(2)}) async-start(s8[8388608]{0:T(1024)(128)(4,1)} %bitcast.76), calls=%async_computation.8 | async-start | bytes 8388608
  195.1 8.4 %collective-permute-start.7 = (f32[128,512]{1,0:T(8,128)S(1)}, f32[128,512]{1,0:T(8,128)S(1)}, u32[]{:S(2)}, u32[]{:S(2)}) collective-permute-start(f32[128,512]{1,0:T(8,128)S(1)} %constant_dynamic-slice_fusion.1), channel_id=1, source_target_pairs={{0,8},{4,12},{8,0},{12,4},{16,24},{20,28},{24,16},{28,20},{1,9},{5... | collective-permute-start | bytes 786440 | tf_op jit(solution)/shard_map/ppermute | solution.py:44
  203.6 5.0 %collective-permute-start.8 = (f32[64,512]{1,0:T(8,128)S(1)}, f32[64,512]{1,0:T(8,128)S(1)}, u32[]{:S(2)}, u32[]{:S(2)}) collective-permute-start(f32[64,512]{1,0:T(8,128)S(1)} %constant_dynamic-slice_fusion), channel_id=1, source_target_pairs={{0,16},{4,20},{8,24},{12,28},{16,0},{20,4},{24,8},{28,12},{1,17},{... | collective-permute-start | bytes 393224 | tf_op jit(solution)/shard_map/ppermute | solution.py:44
  208.6 5.0 %collective-permute-start.9 = (f32[64,512]{1,0:T(8,128)S(1)}, f32[64,512]{1,0:T(8,128)S(1)}, u32[]{:S(2)}, u32[]{:S(2)}) collective-permute-start(f32[64,512]{1,0:T(8,128)S(1)} %dynamic-slice_add_fusion.4), channel_id=1, source_target_pairs={{0,16},{4,20},{8,24},{12,28},{16,0},{20,4},{24,8},{28,12},{1,17},{... | collective-permute-start | bytes 393224 | tf_op jit(solution)/shard_map/ppermute | solution.py:47
  213.7 6.4 %collective-permute-start.10 = (f32[128,512]{1,0:T(8,128)S(1)}, f32[128,512]{1,0:T(8,128)S(1)}, u32[]{:S(2)}, u32[]{:S(2)}) collective-permute-start(f32[128,512]{1,0:T(8,128)S(1)} %pad_maximum_fusion.5), channel_id=1, source_target_pairs={{0,8},{4,12},{8,0},{12,4},{16,24},{20,28},{24,16},{28,20},{1,9},{5... | collective-permute-start | bytes 786440 | tf_op jit(solution)/shard_map/ppermute | solution.py:47
  220.2 2.8 slice-start.3
  220.2 2.0 collective-permute-start.11
  337.1 3.1 copy-start.1
Sparse Core Ops, SparseCore 0:
  13.4 83.4 all-gather.4
  98.5 79.2 all-gather.2
  180.1 75.2 reduce-scatter.2
  257.5 77.2 reduce-scatter.4
where the time goes:
time: 347 us
  waiting for transfers between devices  234 us (67%)
  matrix products  59.9 us (17%)
  between operations  15.9 us (5%)
  starting transfers between devices  13.4 us (4%)
  local copies, waits for them, and re-layouts  13.3 us (4%)
  other arithmetic  10.4 us (3%)
    reduce_scatter x2, waiting for transfers between devices, per_device(): lax.psum_scatter(correction, 'ba', scatter_dimension=1, tiled=True)  94.6 us
    all_gather x2, waiting for transfers between devices, per_device(): every = lax.all_gather(own, 'ba', axis=1, tiled=True)  94.5 us
    dot_general x5, matrix products, mdot(): jnp.dot(left, right, precision=lax.Precision.HIGH, preferred_element_type...  34.9 us
    dot_general x4, matrix products, tdot(): lax.dot_general(left, right, (((0,), (0,)), ((), ())), precision=lax.Prec...  25 us
    ppermute x6, waiting for transfers between devices, sum_over(): block = kept + lax.ppermute(sent, axis, [(i, i ^ bit) for i in range(size)])  24.5 us
    ppermute x6, waiting for transfers between devices, sum_over(): other = lax.ppermute(block, axis, [(i, i ^ bit) for i in range(size)])  20.2 us
  transfers between devices with their start and end apart: 16, of which 16 were waited for; matrix products, arithmetic and copies ran while one was open for 20% of the time, Pallas kernels for 0%

commit v1 on v0

v1 whole, which is shorter than its diff:
```python
import functools

import jax
import jax.numpy as jnp
from jax import lax
from jax.experimental import pallas as pl
from jax.experimental.pallas import tpu as pltpu
from jax.sharding import PartitionSpec as P

MESH = pl.DeviceIdType.MESH
LANES = 128
HALF = LANES // 2
PIECES = 4
TILE = 256
BF16 = jnp.bfloat16
F32 = jnp.float32


def split(value):
    high = value.astype(BF16)
    return high, (value - high.astype(F32)).astype(BF16)


def turned(packed):
    lane = lax.broadcasted_iota(jnp.int32, packed.shape, 1)
    other = pltpu.roll(packed, HALF, axis=1)
    return jnp.where(lane < HALF, other, -other)


def pdot(left, right):
    return jnp.dot(left, right, preferred_element_type=F32)


def kernel(
    G, B, U, K, delay,
    offset_ref, panel_ref, weight_ref, psi_ref, dpsi_ref, out_ref,
    psi_t, psi_w, a_ref, s_ref, c_ref, parts, r_ref, m_ref, acc, x_ref,
    psi_sem, a_send, a_recv, s_send, s_recv, m_send, m_recv,
):
    rows, cols = dpsi_ref.shape[1:]
    nb = psi_ref.shape[2]
    tiles = nb // LANES
    pr = rows // PIECES
    nr = nb // G
    g = lax.axis_index("ga")
    z = lax.axis_index("ba")

    def psi_copies():
        for part in range(2):
            for t in range(tiles):
                i = part * tiles + t
                lanes = pl.ds(t * LANES, LANES)
                yield pltpu.make_async_copy(
                    psi_ref.at[part, :, lanes], c_ref.at[i, pl.ds(0, rows)], psi_sem.at[0, i]
                )
                yield pltpu.make_async_copy(
                    psi_ref.at[part, pl.ds(0, TILE), lanes],
                    c_ref.at[i, pl.ds(rows, TILE)],
                    psi_sem.at[1, i],
                )

    for copy in psi_copies():
        copy.start()

    barrier = pltpu.get_barrier_semaphore()
    for q in range(1, G):
        pl.semaphore_signal(barrier, inc=1, device_id={"ga": lax.rem(g + q, G)}, device_id_type=MESH)

    @pl.when(z > 0)
    def _():
        pl.semaphore_signal(barrier, inc=1, device_id={"ba": z - 1}, device_id_type=MESH)

    @pl.when(z < B - 1)
    def _():
        pl.semaphore_signal(barrier, inc=1, device_id={"ba": z + 1}, device_id_type=MESH)

    pl.semaphore_wait(barrier, G - 1 + jnp.where(z > 0, 1, 0) + jnp.where(z < B - 1, 1, 0))

    def place(lane):
        return z if lane == 0 else B - 1 - z

    def true(lane, index):
        return index if lane == 0 else B - 1 - index

    def piece(p):
        return pl.ds(pl.multiple_of(p * pr, pr), pr)

    def a_copy(lane, unit, p):
        return pltpu.make_async_remote_copy(
            a_ref.at[unit, piece(p)], a_ref.at[unit, piece(p)],
            a_send.at[lane, unit, p], a_recv.at[unit, p],
            device_id={"ba": true(lane, jnp.minimum(place(lane) + 1, B - 1))}, device_id_type=MESH,
        )

    def s_slot(lane, at, dest, u):
        shared = true(lane, dest) * U + u
        if lane == 0:
            return shared
        return jnp.where(dest == at, B * U + u, shared)

    def s_copy(lane, source, unit, slot, p):
        return pltpu.make_async_remote_copy(
            source, s_ref.at[slot, piece(p)], s_send.at[unit, p], s_recv.at[slot, p],
            device_id={"ba": true(lane, jnp.minimum(place(lane) + 1, B - 1))}, device_id_type=MESH,
        )

    def s_wait(slot, p):
        ref = s_ref.at[slot, piece(p)]
        pltpu.make_async_copy(ref, ref, s_recv.at[slot, p]).wait()

    def gathered(lane, k):
        at = place(lane)
        count = U * at
        arrives = (k >= 1) & (k <= count)
        if U == 2:
            index = jnp.where(k <= at, at - k, k - at - 1)
            u = jnp.where(k <= at, 0, 1)
        else:
            index, u = at - k, 0 * k
        own = (2 * at + lane < B) & (k > count) & (k <= count + U)
        index = jnp.where(own, at, index)
        u = jnp.where(own, k - count - 1, u)
        has = arrives | own
        unit = jnp.where(has, true(lane, index) * U + u, 0)
        return arrives, has, unit

    def reduced(lane, k):
        at = place(lane)
        m = k - U * at - delay
        arrives = (at > 0) & (m >= 1) & (m <= U * (B - at))
        if U == 2:
            dest = jnp.where(m <= B - at, at + m - 1, 2 * B - at - m)
            u = jnp.where(m <= B - at, 0, 1)
        else:
            dest, u = at + m - 1, 0 * k
        dest = jnp.where(arrives, dest, at)
        return arrives, dest, u

    for u in range(U):
        for p in range(PIECES):
            span = pl.ds(p * pr, pr)
            own = slice(u * HALF, (u + 1) * HALF)
            a_ref[z * U + u, span, :] = jnp.concatenate(
                [dpsi_ref[0, span, own], dpsi_ref[1, span, own]], axis=1
            )
            if u == 0:
                for lane in range(2):
                    @pl.when(place(lane) < B - 1)
                    def _(lane=lane, p=p):
                        a_copy(lane, z * U, p).start()

    def send_last(lane):
        if U == 2:
            for p in range(PIECES):
                a_copy(lane, z * U + 1, p).start()

    for lane in range(2):
        @pl.when((place(lane) == 0) & (B > 1))
        def _(lane=lane):
            send_last(lane)

    for copy in psi_copies():
        copy.wait()
    offset = offset_ref[g]
    for part in range(2):
        for t in range(tiles):
            i = part * tiles + t
            row = weight_ref[pl.ds(panel_ref[t], 1), :]

            def load(n, carry, i=i, row=row):
                start = lax.rem(n * TILE - offset + rows, rows)
                block = c_ref[i, pl.ds(start, TILE), :]
                span = pl.ds(pl.multiple_of(n * TILE, TILE), TILE)
                bands = slice(i * LANES, (i + 1) * LANES)
                high, rest = split(block.T)
                psi_t[0, bands, span] = high
                psi_t[1, bands, span] = rest
                high, rest = split(block * row)
                psi_w[0, span, bands] = high
                psi_w[1, span, bands] = rest
                return carry

            lax.fori_loop(0, rows // TILE, load, 0)

    def margin(lane, unit, p):
        high, rest = split(a_ref[unit, piece(p), :])
        right = jnp.concatenate([high, rest], axis=1)
        for block in range(0, 2 * nb, TILE):
            bands = slice(block, block + TILE)
            wide = pdot(psi_t[0, bands, piece(p)], right) + pdot(psi_t[1, bands, piece(p)], right)
            narrow = wide[:, :LANES] + wide[:, LANES:]
            acc[lane, bands, :] = jnp.where(p == 0, 0.0, acc[lane, bands, :]) + narrow

    def exchange(lane, unit, phase, start):
        for q in range(1, G):
            peer = lax.rem(g + q, G)
            if phase == 0:
                source = parts.at[lane, pl.ds(pl.multiple_of(peer * nr, nr), nr)]
                target = r_ref.at[unit, q - 1]
            else:
                source = m_ref.at[unit, pl.ds(pl.multiple_of(g * nr, nr), nr)]
                target = source
            pltpu.make_async_remote_copy(
                source, target, m_send.at[phase, unit], m_recv.at[phase, unit],
                device_id={"ga": peer}, device_id_type=MESH,
            ).start()

    def exchange_wait(unit, sem):
        ref = r_ref.at[unit]
        pltpu.make_async_copy(ref, ref, sem).wait()

    def publish(lane, unit):
        parts[lane] = acc[lane, :nb, :] + turned(acc[lane, nb:, :])
        exchange(lane, unit, 0, True)

    def reduce(lane, unit):
        exchange_wait(unit, m_recv.at[0, unit])
        exchange_wait(unit, m_send.at[0, unit])
        mine = pl.ds(pl.multiple_of(g * nr, nr), nr)
        total = parts[lane, mine, :]
        for q in range(1, G):
            total = total + r_ref[unit, q - 1]
        m_ref[unit, mine, :] = total
        exchange(lane, unit, 1, True)

    def collect(lane, unit):
        exchange_wait(unit, m_recv.at[1, unit])
        whole = m_ref[unit]
        high, rest = split(whole)
        x_ref[lane, :nb, :LANES] = high
        x_ref[lane, :nb, LANES:] = rest
        high, rest = split(-turned(whole))
        x_ref[lane, nb:, :LANES] = high
        x_ref[lane, nb:, LANES:] = rest

    def correct(lane, unit, p):
        right = x_ref[lane]
        for block in range(0, pr, TILE):
            span = pl.ds(pl.multiple_of(p * pr + block, TILE), TILE)
            wide = pdot(psi_w[0, span, :], right) + pdot(psi_w[1, span, :], right)
            c_ref[unit, span, :] = wide[:, :LANES] + wide[:, LANES:]

    def step(n, carry):
        k, p = n // PIECES + 1, lax.rem(n, PIECES)
        for lane in range(2):
            at = place(lane)
            arrives, has, unit = gathered(lane, k)

            @pl.when(arrives)
            def _(lane=lane, at=at, unit=unit):
                a_copy(lane, unit, p).wait_recv()

                @pl.when(at < B - 1)
                def _():
                    a_copy(lane, unit, p).start()

            if U == 2:
                @pl.when((at > 0) & (at < B - 1) & (k == U * at) & (p == PIECES - 1))
                def _(lane=lane):
                    send_last(lane)

            arrives, dest, u = reduced(lane, k)

            @pl.when(arrives)
            def _(lane=lane, at=at, dest=dest, u=u):
                slot = s_slot(lane, at, dest, u)
                s_wait(slot, p)

                @pl.when(dest > at)
                def _():
                    unit = true(lane, dest) * U + u
                    s_ref[slot, piece(p), :] = s_ref[slot, piece(p), :] + c_ref[unit, piece(p), :]
                    s_copy(lane, s_ref.at[slot, piece(p)], unit, s_slot(lane, at + 1, dest, u), p).start()

        for lane in range(2):
            _, has, unit = gathered(lane, k - 1)

            @pl.when(has & (p == 0))
            def _(lane=lane, unit=unit):
                reduce(lane, unit)

            @pl.when(has & (p == 1))
            def _(lane=lane, unit=unit):
                collect(lane, unit)

            @pl.when(has & ((p == 1) | (p == 2)))
            def _(lane=lane, unit=unit):
                away = 1 - lane

                def one(i, carry):
                    c = 2 * (p - 1) + i
                    correct(lane, unit, c)

                    @pl.when((place(away) == 0) & (unit // U != z))
                    def _():
                        dest = true(away, unit // U)
                        slot = s_slot(away, 1, dest, lax.rem(unit, U))
                        s_copy(away, c_ref.at[unit, piece(c)], unit, slot, c).start()

                    return carry

                lax.fori_loop(0, PIECES // 2, one, 0)

        for lane in range(2):
            _, has, unit = gathered(lane, k)

            @pl.when(has)
            def _(lane=lane, unit=unit):
                margin(lane, unit, p)

                @pl.when(p == PIECES - 1)
                def _():
                    publish(lane, unit)

        return carry

    lax.fori_loop(0, K * PIECES, step, 0)

    def finish(p, carry):
        sums = []
        for u in range(U):
            unit = z * U + u
            total = c_ref[unit, piece(p), :]
            total = total + jnp.where(z > 0, s_ref[unit, piece(p), :], 0.0)
            total = total + jnp.where(z < B - 1, s_ref[B * U + u, piece(p), :], 0.0)
            sums.append(a_ref[unit, piece(p), :] - total)
        for part in range(2):
            half = slice(part * HALF, (part + 1) * HALF)
            out_ref[part, piece(p), :] = jnp.concatenate([total[:, half] for total in sums], axis=1)
        return carry

    lax.fori_loop(0, PIECES, finish, 0)

    def drain(n, carry):
        unit, p = n // PIECES, lax.rem(n, PIECES)
        block = unit // U

        @pl.when((block <= z) & (z < B - 1))
        def _():
            a_copy(0, unit, p).wait_send()

        @pl.when((block >= z) & (z > 0))
        def _():
            a_copy(1, unit, p).wait_send()

        @pl.when(block != z)
        def _():
            ref = s_ref.at[unit, piece(p)]
            pltpu.make_async_copy(ref, ref, s_send.at[unit, p]).wait()

        @pl.when(p == 0)
        def _():
            exchange_wait(unit, m_send.at[1, unit])

        return carry

    lax.fori_loop(0, B * U * PIECES, drain, 0)


def per_device(G, B, psi, dpsi, band_weight, panel_band, slab_offset):
    _, rows, cols = dpsi.shape
    nb = psi.shape[2]
    U = cols // HALF
    delay = 2 - U
    K = U * B + delay
    units = B * U
    weight = band_weight.reshape(-1, LANES)
    smem = pl.BlockSpec(memory_space=pltpu.SMEM)
    vmem = pl.BlockSpec(memory_space=pltpu.VMEM)
    flops = 2 * 2 * 2 * (2 * nb) * rows * (2 * LANES) * units
    return pl.pallas_call(
        functools.partial(kernel, G, B, U, K, delay),
        out_shape=jax.ShapeDtypeStruct(dpsi.shape, F32),
        in_specs=[smem, smem, vmem, pl.BlockSpec(memory_space=pl.ANY), vmem],
        out_specs=vmem,
        scratch_shapes=[
            pltpu.VMEM((2, 2 * nb, rows), BF16),
            pltpu.VMEM((2, rows, 2 * nb), BF16),
            pltpu.VMEM((units, rows, LANES), F32),
            pltpu.VMEM((units + U, rows, LANES), F32),
            pltpu.VMEM((max(units, 2 * nb // LANES), rows + TILE, LANES), F32),
            pltpu.VMEM((2, nb, LANES), F32),
            pltpu.VMEM((units, G - 1, nb // G, LANES), F32),
            pltpu.VMEM((units, nb, LANES), F32),
            pltpu.VMEM((2, 2 * nb, LANES), F32),
            pltpu.VMEM((2, 2 * nb, 2 * LANES), BF16),
            pltpu.SemaphoreType.DMA((2, 2 * nb // LANES)),
            pltpu.SemaphoreType.DMA((2, units, PIECES)),
            pltpu.SemaphoreType.DMA((units, PIECES)),
            pltpu.SemaphoreType.DMA((units, PIECES)),
            pltpu.SemaphoreType.DMA((units + U, PIECES)),
            pltpu.SemaphoreType.DMA((2, units)),
            pltpu.SemaphoreType.DMA((2, units)),
        ],
        compiler_params=pltpu.CompilerParams(
            collective_id=0, has_side_effects=True, vmem_limit_bytes=67043328
        ),
        cost_estimate=pl.CostEstimate(flops=flops, bytes_accessed=12 << 20, transcendentals=0),
        name="project",
    )(slab_offset, panel_band, weight, psi, dpsi)


def solution(mesh):
    in_specs = (P(None, "ga", "ba"), P(None, "ga", "ba"), P(), P("ba"), P())
    out_specs = P(None, "ga", "ba")
    return jax.shard_map(
        functools.partial(per_device, mesh.shape["ga"], mesh.shape["ba"]),
        mesh=mesh, in_specs=in_specs, out_specs=out_specs, check_vma=False,
    )
```

time: 347 us -> 196 us (0.56)
  waiting for transfers between devices: 234 us -> 0 us
  Pallas kernels: 0 us -> 193 us
  matrix products: 59.9 us -> 0 us
  between operations: 15.9 us -> 0.01 us
  starting transfers between devices: 13.4 us -> 0 us
  other arithmetic: 10.4 us -> 0 us
  local copies, waits for them, and re-layouts: 13.3 us -> 3.05 us
    pallas_call x0 -> x1, Pallas kernels: none -> 193 us  [per_device(): pl.pallas_call(functools.partial(kernel, G, B, U, K, delay), out_shape=ja...]
    reduce_scatter x2 -> x0, waiting for transfers between devices: 94.6 us -> none  [per_device(): lax.psum_scatter(correction, 'ba', scatter_dimension=1, tiled=True)]
    all_gather x2 -> x0, waiting for transfers between devices: 94.5 us -> none  [per_device(): every = lax.all_gather(own, 'ba', axis=1, tiled=True)]
    dot_general x9 -> x0, matrix products: 59.9 us -> none  [the longest x5 34.9 us: mdot(): jnp.dot(left, right, precision=lax.Precision.HIGH, preferred_element_type...]
    ppermute x12 -> x0, waiting for transfers between devices: 44.6 us -> none  [the longest x6 24.5 us: sum_over(): block = kept + lax.ppermute(sent, axis, [(i, i ^ bit) for i in range(size)])]
    ppermute x12 -> x0, starting transfers between devices: 13.3 us -> none  [the longest x6 6.66 us: sum_over(): block = kept + lax.ppermute(sent, axis, [(i, i ^ bit) for i in range(size)])]
    concatenate x8 -> x0, other arithmetic: 5.32 us -> none  [the longest x2 2.09 us: per_device(): jnp.concatenate([aligned[0, :, columns], aligned[1, :, columns]], axis=1)]
    dynamic_slice x8 -> x0, local copies, waits for them, and re-layouts: 4.02 us -> none  [the longest x1 1.81 us: per_device(): return jnp.roll(result, offset, axis=1)]
  transfers between devices with their start and end apart: 16 -> 0, of which waited for: 16 -> 0; matrix products, arithmetic and copies ran while one was open for 20% -> 0% of each run, Pallas kernels for 0% -> 0%
where the time goes in v1:
time: 196 us
  Pallas kernels  193 us (98%)
  local copies, waits for them, and re-layouts  3.05 us (2%)
    pallas_call x1, Pallas kernels, per_device(): pl.pallas_call(functools.partial(kernel, G, B, U, K, delay), out_shape=ja...  193 us

profile of v1, /device:TPU:0, one launch (start us, length us, event | category | flops | bytes accessed | tf_op | source)
XLA Modules:
  0.0 196.1 jit_solution(15295759538566109458)
XLA Ops:
  0.0 193.0 %project.1 = f32[2,2048,128]{2,1,0:T(8,128)} custom-call(s32[8]{0:T(128)} %offset_ref.1, s32[4]{0:T(128)} %panel_ref.1, f32[16,128]{1,0:T(8,128)} %bitcast.1, f32[2,2048,512]{2,1,0:T(8,128)} %psi_ref.1, f32[2,2048,128]{2,1,0:T(8,128)} %dpsi_ref.1), custom_call_target="tpu_custom_call" | custom-call | flops 34359738368 | bytes 12582912 | tf_op jit(solution)/shard_map/project/pallas_call | solution.py:371
  193.0 3.0 %copy.7 = f32[2,2048,128]{2,1,0:T(8,128)} copy(f32[2,2048,128]{2,1,0:T(8,128)} %project.1) | data formatting | bytes 4194304

commit v2 on v1

--- a/solution.py
+++ b/solution.py
@@ -35,7 +35,7 @@
     G, B, U, K, delay,
     offset_ref, panel_ref, weight_ref, psi_ref, dpsi_ref, out_ref,
     psi_t, psi_w, a_ref, s_ref, c_ref, parts, r_ref, m_ref, acc, x_ref,
-    psi_sem, a_send, a_recv, s_send, s_recv, m_send, m_recv,
+    psi_sem, dpsi_sem, a_send, a_recv, s_send, s_recv, m_send, m_recv,
 ):
     rows, cols = dpsi_ref.shape[1:]
     nb = psi_ref.shape[2]
@@ -59,6 +59,12 @@
                     psi_sem.at[1, i],
                 )
 
+    def dpsi_copy(p):
+        span = pl.ds(p * pr, pr)
+        return pltpu.make_async_copy(dpsi_ref.at[:, span], out_ref.at[:, span], dpsi_sem.at[p])
+
+    for p in range(PIECES):
+        dpsi_copy(p).start()
     for copy in psi_copies():
         copy.start()
 
@@ -136,18 +142,23 @@
         dest = jnp.where(arrives, dest, at)
         return arrives, dest, u
 
-    for u in range(U):
+    def pack(u, p):
+        span = pl.ds(p * pr, pr)
+        own = slice(u * HALF, (u + 1) * HALF)
+        a_ref[z * U + u, span, :] = jnp.concatenate(
+            [out_ref[0, span, own], out_ref[1, span, own]], axis=1
+        )
+
+    for p in range(PIECES):
+        dpsi_copy(p).wait()
+        pack(0, p)
+        for lane in range(2):
+            @pl.when(place(lane) < B - 1)
+            def _(lane=lane, p=p):
+                a_copy(lane, z * U, p).start()
+    for u in range(1, U):
         for p in range(PIECES):
-            span = pl.ds(p * pr, pr)
-            own = slice(u * HALF, (u + 1) * HALF)
-            a_ref[z * U + u, span, :] = jnp.concatenate(
-                [dpsi_ref[0, span, own], dpsi_ref[1, span, own]], axis=1
-            )
-            if u == 0:
-                for lane in range(2):
-                    @pl.when(place(lane) < B - 1)
-                    def _(lane=lane, p=p):
-                        a_copy(lane, z * U, p).start()
+            pack(u, p)
 
     def send_last(lane):
         if U == 2:
@@ -240,83 +251,7 @@
             wide = pdot(psi_w[0, span, :], right) + pdot(psi_w[1, span, :], right)
             c_ref[unit, span, :] = wide[:, :LANES] + wide[:, LANES:]
 
-    def step(n, carry):
-        k, p = n // PIECES + 1, lax.rem(n, PIECES)
-        for lane in range(2):
-            at = place(lane)
-            arrives, has, unit = gathered(lane, k)
-
-            @pl.when(arrives)
-            def _(lane=lane, at=at, unit=unit):
-                a_copy(lane, unit, p).wait_recv()
-
-                @pl.when(at < B - 1)
-                def _():
-                    a_copy(lane, unit, p).start()
-
-            if U == 2:
-                @pl.when((at > 0) & (at < B - 1) & (k == U * at) & (p == PIECES - 1))
-                def _(lane=lane):
-                    send_last(lane)
-
-            arrives, dest, u = reduced(lane, k)
-
-            @pl.when(arrives)
-            def _(lane=lane, at=at, dest=dest, u=u):
-                slot = s_slot(lane, at, dest, u)
-                s_wait(slot, p)
-
-                @pl.when(dest > at)
-                def _():
-                    unit = true(lane, dest) * U + u
-                    s_ref[slot, piece(p), :] = s_ref[slot, piece(p), :] + c_ref[unit, piece(p), :]
-                    s_copy(lane, s_ref.at[slot, piece(p)], unit, s_slot(lane, at + 1, dest, u), p).start()
-
-        for lane in range(2):
-            _, has, unit = gathered(lane, k - 1)
-
-            @pl.when(has & (p == 0))
-            def _(lane=lane, unit=unit):
-                reduce(lane, unit)
-
-            @pl.when(has & (p == 1))
-            def _(lane=lane, unit=unit):
-                collect(lane, unit)
-
-            @pl.when(has & ((p == 1) | (p == 2)))
-            def _(lane=lane, unit=unit):
-                away = 1 - lane
-
-                def one(i, carry):
-                    c = 2 * (p - 1) + i
-                    correct(lane, unit, c)
-
-                    @pl.when((place(away) == 0) & (unit // U != z))
-                    def _():
-                        dest = true(away, unit // U)
-                        slot = s_slot(away, 1, dest, lax.rem(unit, U))
-                        s_copy(away, c_ref.at[unit, piece(c)], unit, slot, c).start()
-
-                    return carry
-
-                lax.fori_loop(0, PIECES // 2, one, 0)
-
-        for lane in range(2):
-            _, has, unit = gathered(lane, k)
-
-            @pl.when(has)
-            def _(lane=lane, unit=unit):
-                margin(lane, unit, p)
-
-                @pl.when(p == PIECES - 1)
-                def _():
-                    publish(lane, unit)
-
-        return carry
-
-    lax.fori_loop(0, K * PIECES, step, 0)
-
-    def finish(p, carry):
+    def finish(p):
         sums = []
         for u in range(U):
             unit = z * U + u
@@ -327,9 +262,86 @@
         for part in range(2):
             half = slice(part * HALF, (part + 1) * HALF)
             out_ref[part, piece(p), :] = jnp.concatenate([total[:, half] for total in sums], axis=1)
+
+    def step(n, carry):
+        k, p = n // PIECES + 1, lax.rem(n, PIECES)
+        for lane in range(2):
+            at = place(lane)
+            arrives, has, unit = gathered(lane, k)
+
+            @pl.when(arrives)
+            def _(lane=lane, at=at, unit=unit):
+                a_copy(lane, unit, p).wait_recv()
+
+                @pl.when(at < B - 1)
+                def _():
+                    a_copy(lane, unit, p).start()
+
+            if U == 2:
+                @pl.when((at > 0) & (at < B - 1) & (k == U * at) & (p == PIECES - 1))
+                def _(lane=lane):
+                    send_last(lane)
+
+            arrives, dest, u = reduced(lane, k)
+
+            @pl.when(arrives)
+            def _(lane=lane, at=at, dest=dest, u=u):
+                slot = s_slot(lane, at, dest, u)
+                s_wait(slot, p)
+
+                @pl.when(dest > at)
+                def _():
+                    unit = true(lane, dest) * U + u
+                    s_ref[slot, piece(p), :] = s_ref[slot, piece(p), :] + c_ref[unit, piece(p), :]
+                    s_copy(lane, s_ref.at[slot, piece(p)], unit, s_slot(lane, at + 1, dest, u), p).start()
+
+        for lane in range(2):
+            _, has, unit = gathered(lane, k - 1)
+
+            @pl.when(has & (p == 0))
+            def _(lane=lane, unit=unit):
+                reduce(lane, unit)
+
+            @pl.when(has & (p == 1))
+            def _(lane=lane, unit=unit):
+                collect(lane, unit)
+
+            @pl.when(has & ((p == 1) | (p == 2)))
+            def _(lane=lane, unit=unit):
+                away = 1 - lane
+
+                def one(i, carry):
+                    c = 2 * (p - 1) + i
+                    correct(lane, unit, c)
+
+                    @pl.when((place(away) == 0) & (unit // U != z))
+                    def _():
+                        dest = true(away, unit // U)
+                        slot = s_slot(away, 1, dest, lax.rem(unit, U))
+                        s_copy(away, c_ref.at[unit, piece(c)], unit, slot, c).start()
+
+                    return carry
+
+                lax.fori_loop(0, PIECES // 2, one, 0)
+
+        for lane in range(2):
+            _, has, unit = gathered(lane, k)
+
+            @pl.when(has)
+            def _(lane=lane, unit=unit):
+                margin(lane, unit, p)
+
+                @pl.when(p == PIECES - 1)
+                def _():
+                    publish(lane, unit)
+
+        @pl.when(k == K)
+        def _():
+            finish(p)
+
         return carry
 
-    lax.fori_loop(0, PIECES, finish, 0)
+    lax.fori_loop(0, K * PIECES, step, 0)
 
     def drain(n, carry):
         unit, p = n // PIECES, lax.rem(n, PIECES)
@@ -367,11 +379,13 @@
     weight = band_weight.reshape(-1, LANES)
     smem = pl.BlockSpec(memory_space=pltpu.SMEM)
     vmem = pl.BlockSpec(memory_space=pltpu.VMEM)
+    hbm = pl.BlockSpec(memory_space=pl.ANY)
+    small = [pltpu.with_memory_space_constraint(x, pltpu.HBM) for x in (slab_offset, panel_band, weight)]
     flops = 2 * 2 * 2 * (2 * nb) * rows * (2 * LANES) * units
     return pl.pallas_call(
         functools.partial(kernel, G, B, U, K, delay),
-        out_shape=jax.ShapeDtypeStruct(dpsi.shape, F32),
-        in_specs=[smem, smem, vmem, pl.BlockSpec(memory_space=pl.ANY), vmem],
+        out_shape=pltpu.VMEM(dpsi.shape, F32),
+        in_specs=[smem, smem, vmem, hbm, hbm],
         out_specs=vmem,
         scratch_shapes=[
             pltpu.VMEM((2, 2 * nb, rows), BF16),
@@ -385,6 +399,7 @@
             pltpu.VMEM((2, 2 * nb, LANES), F32),
             pltpu.VMEM((2, 2 * nb, 2 * LANES), BF16),
             pltpu.SemaphoreType.DMA((2, 2 * nb // LANES)),
+            pltpu.SemaphoreType.DMA((PIECES,)),
             pltpu.SemaphoreType.DMA((2, units, PIECES)),
             pltpu.SemaphoreType.DMA((units, PIECES)),
             pltpu.SemaphoreType.DMA((units, PIECES)),
@@ -393,11 +408,11 @@
             pltpu.SemaphoreType.DMA((2, units)),
         ],
         compiler_params=pltpu.CompilerParams(
-            collective_id=0, has_side_effects=True, vmem_limit_bytes=67043328
+            collective_id=0, has_side_effects=True, vmem_limit_bytes=60000000
         ),
         cost_estimate=pl.CostEstimate(flops=flops, bytes_accessed=12 << 20, transcendentals=0),
         name="project",
-    )(slab_offset, panel_band, weight, psi, dpsi)
+    )(*small, psi, dpsi)
 
 
 def solution(mesh):

time: 196 us -> 192 us (0.980)
  Pallas kernels: 193 us -> 191 us
    pallas_call x1, Pallas kernels: 193 us -> 191 us  [per_device(): pl.pallas_call(functools.partial(kernel, G, B, U, K, delay), out_shape=pl...]
where the time goes in v2:
time: 192 us
  Pallas kernels  191 us (99%)
    pallas_call x1, Pallas kernels, per_device(): pl.pallas_call(functools.partial(kernel, G, B, U, K, delay), out_shape=pl...  191 us

profile of v2, /device:TPU:0, one launch (start us, length us, event | category | flops | bytes accessed | tf_op | source)
XLA Modules:
  0.0 191.9 jit_solution(6193300141472958349)
XLA Ops:
  0.0 190.5 %project.1 = f32[2,2048,128]{2,1,0:T(8,128)S(1)} custom-call(s32[8]{0:T(128)} %offset_ref.1, s32[4]{0:T(128)} %panel_ref.1, f32[16,128]{1,0:T(8,128)} %bitcast.1, f32[2,2048,512]{2,1,0:T(8,128)} %psi_ref.1, f32[2,2048,128]{2,1,0:T(8,128)} %dpsi_ref.1), custom_call_target="tpu_custom_call" | custom-call | flops 34359738368 | bytes 12582912 | tf_op jit(solution)/shard_map/project/pallas_call | solution.py:385
  190.6 1.3 copy.7

commit v3 on v2

--- a/solution.py
+++ b/solution.py
@@ -65,8 +65,6 @@
 
     for p in range(PIECES):
         dpsi_copy(p).start()
-    for copy in psi_copies():
-        copy.start()
 
     barrier = pltpu.get_barrier_semaphore()
     for q in range(1, G):
@@ -156,6 +154,8 @@
             @pl.when(place(lane) < B - 1)
             def _(lane=lane, p=p):
                 a_copy(lane, z * U, p).start()
+    for copy in psi_copies():
+        copy.start()
     for u in range(1, U):
         for p in range(PIECES):
             pack(u, p)
@@ -170,28 +170,32 @@
         def _(lane=lane):
             send_last(lane)
 
-    for copy in psi_copies():
-        copy.wait()
-    offset = offset_ref[g]
-    for part in range(2):
-        for t in range(tiles):
-            i = part * tiles + t
-            row = weight_ref[pl.ds(panel_ref[t], 1), :]
-
-            def load(n, carry, i=i, row=row):
-                start = lax.rem(n * TILE - offset + rows, rows)
-                block = c_ref[i, pl.ds(start, TILE), :]
-                span = pl.ds(pl.multiple_of(n * TILE, TILE), TILE)
-                bands = slice(i * LANES, (i + 1) * LANES)
-                high, rest = split(block.T)
-                psi_t[0, bands, span] = high
-                psi_t[1, bands, span] = rest
-                high, rest = split(block * row)
-                psi_w[0, span, bands] = high
-                psi_w[1, span, bands] = rest
-                return carry
-
-            lax.fori_loop(0, rows // TILE, load, 0)
+    def prepare(p):
+        @pl.when(p == 0)
+        def _():
+            for copy in psi_copies():
+                copy.wait()
+
+        offset = offset_ref[g]
+        for part in range(2):
+            for t in range(tiles):
+                i = part * tiles + t
+                row = weight_ref[pl.ds(panel_ref[t], 1), :]
+
+                def load(n, carry, i=i, row=row):
+                    at = p * pr + n * TILE
+                    block = c_ref[i, pl.ds(lax.rem(at - offset + rows, rows), TILE), :]
+                    span = pl.ds(pl.multiple_of(at, TILE), TILE)
+                    bands = slice(i * LANES, (i + 1) * LANES)
+                    high, rest = split(block.T)
+                    psi_t[0, bands, span] = high
+                    psi_t[1, bands, span] = rest
+                    high, rest = split(block * row)
+                    psi_w[0, span, bands] = high
+                    psi_w[1, span, bands] = rest
+                    return carry
+
+                lax.fori_loop(0, pr // TILE, load, 0)
 
     def margin(lane, unit, p):
         high, rest = split(a_ref[unit, piece(p), :])
@@ -263,6 +267,21 @@
             half = slice(part * HALF, (part + 1) * HALF)
             out_ref[part, piece(p), :] = jnp.concatenate([total[:, half] for total in sums], axis=1)
 
+    def summed(lane, k, p):
+        at = place(lane)
+        arrives, dest, u = reduced(lane, k)
+
+        @pl.when(arrives)
+        def _():
+            slot = s_slot(lane, at, dest, u)
+            s_wait(slot, p)
+
+            @pl.when(dest > at)
+            def _():
+                unit = true(lane, dest) * U + u
+                s_ref[slot, piece(p), :] = s_ref[slot, piece(p), :] + c_ref[unit, piece(p), :]
+                s_copy(lane, s_ref.at[slot, piece(p)], unit, s_slot(lane, at + 1, dest, u), p).start()
+
     def step(n, carry):
         k, p = n // PIECES + 1, lax.rem(n, PIECES)
         for lane in range(2):
@@ -282,18 +301,11 @@
                 def _(lane=lane):
                     send_last(lane)
 
-            arrives, dest, u = reduced(lane, k)
-
-            @pl.when(arrives)
-            def _(lane=lane, at=at, dest=dest, u=u):
-                slot = s_slot(lane, at, dest, u)
-                s_wait(slot, p)
-
-                @pl.when(dest > at)
-                def _():
-                    unit = true(lane, dest) * U + u
-                    s_ref[slot, piece(p), :] = s_ref[slot, piece(p), :] + c_ref[unit, piece(p), :]
-                    s_copy(lane, s_ref.at[slot, piece(p)], unit, s_slot(lane, at + 1, dest, u), p).start()
+            summed(lane, k, p)
+
+        @pl.when(k == 1)
+        def _():
+            prepare(p)
 
         for lane in range(2):
             _, has, unit = gathered(lane, k - 1)
@@ -335,13 +347,17 @@
                 def _():
                     publish(lane, unit)
 
-        @pl.when(k == K)
-        def _():
-            finish(p)
-
         return carry
 
-    lax.fori_loop(0, K * PIECES, step, 0)
+    lax.fori_loop(0, (K - 1) * PIECES, step, 0)
+
+    def last(p, carry):
+        for lane in range(2):
+            summed(lane, K, p)
+        finish(p)
+        return carry
+
+    lax.fori_loop(0, PIECES - 1, last, 0)
 
     def drain(n, carry):
         unit, p = n // PIECES, lax.rem(n, PIECES)
@@ -367,6 +383,7 @@
         return carry
 
     lax.fori_loop(0, B * U * PIECES, drain, 0)
+    last(PIECES - 1, 0)
 
 
 def per_device(G, B, psi, dpsi, band_weight, panel_band, slab_offset):
@@ -374,7 +391,7 @@
     nb = psi.shape[2]
     U = cols // HALF
     delay = 2 - U
-    K = U * B + delay
+    K = U * B + 2 * delay
     units = B * U
     weight = band_weight.reshape(-1, LANES)
     smem = pl.BlockSpec(memory_space=pltpu.SMEM)

time: 192 us -> 191 us (level)
  Pallas kernels: 191 us -> 189 us
where the time goes in v3:
time: 191 us
  Pallas kernels  189 us (99%)
    pallas_call x1, Pallas kernels, per_device(): pl.pallas_call(functools.partial(kernel, G, B, U, K, delay), out_shape=pl...  189 us

profile of v3, /device:TPU:0, one launch (start us, length us, event | category | flops | bytes accessed | tf_op | source)
XLA Modules:
  0.0 190.6 jit_solution(3748586576740614562)
XLA Ops:
  0.0 189.3 %project.1 = f32[2,2048,128]{2,1,0:T(8,128)S(1)} custom-call(s32[8]{0:T(128)} %offset_ref.1, s32[4]{0:T(128)} %panel_ref.1, f32[16,128]{1,0:T(8,128)} %bitcast.1, f32[2,2048,512]{2,1,0:T(8,128)} %psi_ref.1, f32[2,2048,128]{2,1,0:T(8,128)} %dpsi_ref.1), custom_call_target="tpu_custom_call" | custom-call | flops 34359738368 | bytes 12582912 | tf_op jit(solution)/shard_map/project/pallas_call | solution.py:402
  189.3 1.3 copy.7

commit v4 on v3

--- a/solution.py
+++ b/solution.py
@@ -67,9 +67,6 @@
         dpsi_copy(p).start()
 
     barrier = pltpu.get_barrier_semaphore()
-    for q in range(1, G):
-        pl.semaphore_signal(barrier, inc=1, device_id={"ga": lax.rem(g + q, G)}, device_id_type=MESH)
-
     @pl.when(z > 0)
     def _():
         pl.semaphore_signal(barrier, inc=1, device_id={"ba": z - 1}, device_id_type=MESH)
@@ -78,7 +75,8 @@
     def _():
         pl.semaphore_signal(barrier, inc=1, device_id={"ba": z + 1}, device_id_type=MESH)
 
-    pl.semaphore_wait(barrier, G - 1 + jnp.where(z > 0, 1, 0) + jnp.where(z < B - 1, 1, 0))
+    for q in range(1, G):
+        pl.semaphore_signal(barrier, inc=1, device_id={"ga": lax.rem(g + q, G)}, device_id_type=MESH)
 
     def place(lane):
         return z if lane == 0 else B - 1 - z
@@ -150,6 +148,8 @@
     for p in range(PIECES):
         dpsi_copy(p).wait()
         pack(0, p)
+        if p == 0:
+            pl.semaphore_wait(barrier, G - 1 + jnp.where(z > 0, 1, 0) + jnp.where(z < B - 1, 1, 0))
         for lane in range(2):
             @pl.when(place(lane) < B - 1)
             def _(lane=lane, p=p):

time: 191 us -> 191 us (level)
  no operation moved by 1% of the time
where the time goes in v4:
time: 191 us
  Pallas kernels  189 us (99%)
    pallas_call x1, Pallas kernels, per_device(): pl.pallas_call(functools.partial(kernel, G, B, U, K, delay), out_shape=pl...  189 us

profile of v4, /device:TPU:0, one launch (start us, length us, event | category | flops | bytes accessed | tf_op | source)
XLA Modules:
  0.0 190.5 jit_solution(14960022126154321797)
XLA Ops:
  0.0 189.2 %project.1 = f32[2,2048,128]{2,1,0:T(8,128)S(1)} custom-call(s32[8]{0:T(128)} %offset_ref.1, s32[4]{0:T(128)} %panel_ref.1, f32[16,128]{1,0:T(8,128)} %bitcast.1, f32[2,2048,512]{2,1,0:T(8,128)} %psi_ref.1, f32[2,2048,128]{2,1,0:T(8,128)} %dpsi_ref.1), custom_call_target="tpu_custom_call" | custom-call | flops 34359738368 | bytes 12582912 | tf_op jit(solution)/shard_map/project/pallas_call | solution.py:402
  189.2 1.3 copy.7

commit v5 on v4

--- a/solution.py
+++ b/solution.py
@@ -255,14 +255,21 @@
             wide = pdot(psi_w[0, span, :], right) + pdot(psi_w[1, span, :], right)
             c_ref[unit, span, :] = wide[:, :LANES] + wide[:, LANES:]
 
-    def finish(p):
-        sums = []
+    def arrived(u, p):
+        lower = jnp.where(z > 0, s_ref[z * U + u, piece(p), :], 0.0)
+        return lower + jnp.where(z < B - 1, s_ref[B * U + u, piece(p), :], 0.0)
+
+    def settle(p, carry):
         for u in range(U):
             unit = z * U + u
-            total = c_ref[unit, piece(p), :]
-            total = total + jnp.where(z > 0, s_ref[unit, piece(p), :], 0.0)
-            total = total + jnp.where(z < B - 1, s_ref[B * U + u, piece(p), :], 0.0)
-            sums.append(a_ref[unit, piece(p), :] - total)
+            kept = a_ref[unit, piece(p), :] - c_ref[unit, piece(p), :]
+            c_ref[unit, piece(p), :] = kept - arrived(u, p) if u < 1 else kept
+        return carry
+
+    def finish(p):
+        sums = [c_ref[z * U + u, piece(p), :] for u in range(U)]
+        if U == 2:
+            sums[1] = sums[1] - arrived(1, p)
         for part in range(2):
             half = slice(part * HALF, (part + 1) * HALF)
             out_ref[part, piece(p), :] = jnp.concatenate([total[:, half] for total in sums], axis=1)
@@ -350,6 +357,7 @@
         return carry
 
     lax.fori_loop(0, (K - 1) * PIECES, step, 0)
+    lax.fori_loop(0, PIECES, settle, 0)
 
     def last(p, carry):
         for lane in range(2):

time: 191 us -> 191 us (level)
  no operation moved by 1% of the time
where the time goes in v5:
time: 191 us
  Pallas kernels  189 us (99%)
    pallas_call x1, Pallas kernels, per_device(): pl.pallas_call(functools.partial(kernel, G, B, U, K, delay), out_shape=pl...  189 us

profile of v5, /device:TPU:0, one launch (start us, length us, event | category | flops | bytes accessed | tf_op | source)
XLA Modules:
  0.0 190.5 jit_solution(6928336464038660001)
XLA Ops:
  0.0 189.2 %project.1 = f32[2,2048,128]{2,1,0:T(8,128)S(1)} custom-call(s32[8]{0:T(128)} %offset_ref.1, s32[4]{0:T(128)} %panel_ref.1, f32[16,128]{1,0:T(8,128)} %bitcast.1, f32[2,2048,512]{2,1,0:T(8,128)} %psi_ref.1, f32[2,2048,128]{2,1,0:T(8,128)} %dpsi_ref.1), custom_call_target="tpu_custom_call" | custom-call | flops 34359738368 | bytes 12582912 | tf_op jit(solution)/shard_map/project/pallas_call | solution.py:410
  189.2 1.3 copy.7
